TPU v7x, 32 devices: a whole 2x2x4 slice. The times are simulated.
32 devices in a mesh: dp: 8 (over z, y), tensor: 4 (over x, core).
Axes of the slice: x: 2, y: 2, z: 4, core: 2. Of those that a mesh axis runs over, the one named last changes fastest.
Arguments:
- hidden_in: bfloat16 [16384, 1024], P(('dp', 'tensor')), may hold values from -6 to 6
- doc_ids: int32 [32, 512], P('dp'), may hold values from 0 to 5, never falling along the last dimension, each value on 1 to 256 neighbouring positions
- unit_slot: int32 [24], replicated, may hold values from 0 to 31, as said below
- masters: float32 [32, 1024, 1024], P('dp', None, 'tensor')
- first_moment: float32 [32, 1024, 1024], P('dp', None, 'tensor')
- second_moment: float32 [32, 1024, 1024], P('dp', None, 'tensor')
- column_state: float32 [3, 2, 6, 1024], P(None, None, None, 'tensor')
- row_state: float32 [3, 2, 6, 1024], replicated
- out_grad: bfloat16 [16384, 1024], P(('dp', 'tensor')), may hold values from -0.046875 to 0.046875
Outputs:
- block_out: float32 [16384, 1024], P(('dp', 'tensor'))
- input_grad: float32 [16384, 1024], P(('dp', 'tensor'))
- unit_master: float32 [32, 1024, 1024], P('dp', None, 'tensor')
- unit_state: float32 [2, 32, 1024, 1024], P(None, 'dp', None, 'tensor')
- column_out: float32 [4, 2, 6, 1024], P(None, None, None, 'tensor')
- row_out: float32 [4, 2, 6, 1024], replicated
Inputs may be any that keep to these rules, and one draw needn't show every extreme that they name: `doc_ids`: within a row the ids never fall; each of the 6 documents covers 1 to 256 tokens, one exactly that many. `unit_slot`: all 24 entries differ; slot s belongs to index s // 4 of dp; some index of dp holds exactly 4 matrices.
All inputs are finite; a program needn't handle non-finite values.
Results may differ from a plain program's by a relative error of at most 0.028.
Values may be sent and summed in bfloat16 or wider, within the bound.
A program may use at most 256 MiB of HBM per device.

v0:
```python
import math
import jax
import jax.numpy as jnp
from jax import lax
from jax.sharding import PartitionSpec as P

HEAD_DIM = 64
LAYERS = 2
STEP = 3
EPS_NORM = 1e-06
RATE_UNITS = 0.05
RATE_SMALL = 0.2
WEIGHT_DECAY = 0.01
ADAM_EPS = 1e-08
BETA_MOMENT = 0.5
BOTH = ("dp", "tensor")


def norm_forward(summed, gain, shift):
    row_mean = jnp.mean(summed, axis=1, keepdims=True)
    centred = summed - row_mean
    inverse = lax.rsqrt(jnp.mean(centred * centred, axis=1, keepdims=True) + EPS_NORM)
    scaled = centred * inverse
    return (scaled * gain + shift, scaled, inverse)


def norm_backward(upstream, scaled, inverse, gain):
    d_scaled = upstream * gain
    mean_one = jnp.mean(d_scaled, axis=1, keepdims=True)
    mean_two = jnp.mean(d_scaled * scaled, axis=1, keepdims=True)
    grad_input = inverse * (d_scaled - mean_one - scaled * mean_two)
    return (grad_input, jnp.sum(upstream * scaled, axis=0), jnp.sum(upstream, axis=0))


def gelu_pair(v):
    z = jnp.abs(v) * 2.0 ** (-0.5)
    t = 1.0 / (1.0 + 0.5 * z)
    poly = 0.17087277
    for coefficient in (
        -0.82215223,
        1.48851587,
        -1.13520398,
        0.27886807,
        -0.18628806,
        0.09678418,
        0.37409196,
        1.00002368,
        -1.26551223,
    ):
        poly = poly * t + coefficient
    bell = jnp.exp(-0.5 * v * v)
    tail = 0.5 * t * jnp.exp(poly) * bell
    cdf = jnp.where(v >= 0.0, 1.0 - tail, tail)
    return (v * cdf, cdf + v * bell * (2.0 * math.pi) ** (-0.5))


def adamw_update(old_value, gradient, first_old, second_old, learn_rate):
    first_new = BETA_MOMENT * first_old + (1.0 - BETA_MOMENT) * gradient
    second_new = BETA_MOMENT * second_old + (1.0 - BETA_MOMENT) * gradient * gradient
    correct = 1.0 - BETA_MOMENT**STEP
    step_size = first_new / correct / (jnp.sqrt(second_new / correct) + ADAM_EPS)
    return (old_value - learn_rate * (step_size + WEIGHT_DECAY * old_value), first_new, second_new)


def dot(left, right, dims):
    return lax.dot_general(left, right, (dims, ((), ())), preferred_element_type=jnp.float32)


def local(
    hidden_in,
    doc_ids,
    unit_slot,
    masters,
    first_moment,
    second_moment,
    column_state,
    row_state,
    out_grad,
):
    slot_count, width, col_width = masters.shape
    units = unit_slot.shape[0]
    per_layer = units // LAYERS
    blocks = (per_layer - 4) // 2
    dp_size = lax.axis_size("dp")
    tensor_size = lax.axis_size("tensor")
    devices = dp_size * tensor_size
    slots = slot_count * dp_size
    rows = hidden_in.shape[0]
    seq_len = doc_ids.shape[1]
    heads = width // HEAD_DIM
    piece = width // devices
    share = seq_len // rows
    tensor_index = lax.axis_index("tensor")
    groups = [list(range(i, i + share)) for i in range(0, tensor_size, share)]
    score_scale = HEAD_DIM ** (-0.5)
    sent = masters.astype(jnp.bfloat16).reshape(slot_count, devices, piece, col_width)
    spread = lax.all_to_all(sent.transpose(1, 0, 2, 3), BOTH, 0, 0)
    spread = spread.reshape(dp_size, tensor_size, slot_count, piece, col_width)
    spread = spread.transpose(0, 2, 3, 1, 4).reshape(slots, piece, width)
    mine = spread[unit_slot]
    layer_mats = []
    for layer in range(LAYERS):
        own = mine[layer * per_layer : (layer + 1) * per_layer].transpose(1, 0, 2)
        full = lax.all_gather(own.reshape(piece, per_layer * width), BOTH, axis=0, tiled=True)
        layer_mats.append(
            (
                full[:, : 3 * width],
                full[:, 3 * width : 4 * width],
                full[:, 4 * width : (4 + blocks) * width],
                full[:, (4 + blocks) * width :],
            )
        )
    row_docs = lax.dynamic_slice_in_dim(doc_ids, tensor_index // share, 1, axis=0)[0]
    my_docs = lax.dynamic_slice_in_dim(row_docs, tensor_index % share * rows, rows)
    same_doc = (my_docs[:, None] == row_docs[None, :])[None]

    def whole_row(value):
        if share == 1:
            return value
        return lax.all_gather(value, "tensor", axis=0, tiled=True, axis_index_groups=groups)

    def own_rows(value):
        if share == 1:
            return value
        return lax.psum_scatter(
            value, "tensor", scatter_dimension=0, tiled=True, axis_index_groups=groups
        )

    col_full = lax.all_gather(column_state[0], "tensor", axis=2, tiled=True)
    hidden = hidden_in.astype(jnp.float32)
    saved_layers = []
    for layer in range(LAYERS):
        w_qkv, w_proj, w_in, w_out = layer_mats[layer]
        row_now = row_state[0, layer]
        col_now = col_full[layer]
        hidden_bf = hidden.astype(jnp.bfloat16)
        mixed = dot(hidden_bf, w_qkv, ((1,), (0,)))
        query = (mixed[:, :width] + col_now[0]).astype(jnp.bfloat16)
        key = whole_row(mixed[:, width : 2 * width].astype(jnp.bfloat16))
        value = whole_row((mixed[:, 2 * width :] + col_now[1]).astype(jnp.bfloat16))
        query = query.reshape(rows, heads, HEAD_DIM)
        key = key.reshape(seq_len, heads, HEAD_DIM)
        value = value.reshape(seq_len, heads, HEAD_DIM)
        scores = (
            jnp.einsum("qhd,khd->hqk", query, key, preferred_element_type=jnp.float32) * score_scale
        )
        scores = jnp.where(same_doc, scores, -1e30)
        row_top = jnp.max(scores, axis=-1, keepdims=True)
        log_total = row_top + jnp.log(jnp.sum(jnp.exp(scores - row_top), axis=-1, keepdims=True))
        soft_bf = jnp.exp(scores - log_total).astype(jnp.bfloat16)
        context = jnp.einsum("hqk,khd->qhd", soft_bf, value, preferred_element_type=jnp.float32)
        context = context.reshape(rows, width).astype(jnp.bfloat16)
        attended = dot(context, w_proj, ((1,), (1,)))
        normed, scaled_one, inverse_one = norm_forward(
            hidden + attended + row_now[0], row_now[2], row_now[3]
        )
        normed_bf = normed.astype(jnp.bfloat16)
        pre_act = dot(normed_bf, w_in, ((1,), (0,))) + col_now[2:].reshape(-1)
        activated, slope = gelu_pair(pre_act)
        activated = activated.astype(jnp.bfloat16)
        slope = slope.astype(jnp.bfloat16)
        mlp_out = dot(activated, w_out, ((1,), (1,)))
        output, scaled_two, inverse_two = norm_forward(
            normed + mlp_out + row_now[1], row_now[4], row_now[5]
        )
        saved_layers.append(
            (hidden_bf, query, key, value, log_total, context, scaled_one, inverse_one, normed_bf)
            + (slope, activated, scaled_two, inverse_two)
        )
        hidden = output
    upstream = out_grad.astype(jnp.float32)
    pieces = [None] * LAYERS
    col_parts = [None] * LAYERS
    row_parts = [None] * LAYERS
    for layer in reversed(range(LAYERS)):
        w_qkv, w_proj, w_in, w_out = layer_mats[layer]
        row_now = row_state[0, layer]
        (
            hidden_bf,
            query,
            key,
            value,
            log_total,
            context,
            scaled_one,
            inverse_one,
            normed_bf,
            slope,
            activated,
            scaled_two,
            inverse_two,
        ) = saved_layers[layer]
        d_two, gain_two, shift_two = norm_backward(upstream, scaled_two, inverse_two, row_now[4])
        grad_bias_two = jnp.sum(d_two, axis=0)
        d_two_bf = d_two.astype(jnp.bfloat16)
        grad_w_out = dot(d_two_bf, activated, ((0,), (0,)))
        d_pre = (dot(d_two_bf, w_out, ((1,), (0,))) * slope).astype(jnp.bfloat16)
        grad_bias_in = jnp.sum(d_pre, axis=0, dtype=jnp.float32)
        grad_w_in = dot(normed_bf, d_pre, ((0,), (0,)))
        d_normed = d_two + dot(d_pre, w_in, ((1,), (1,)))
        d_one, gain_one, shift_one = norm_backward(d_normed, scaled_one, inverse_one, row_now[2])
        grad_bias_proj = jnp.sum(d_one, axis=0)
        d_one_bf = d_one.astype(jnp.bfloat16)
        grad_w_proj = dot(d_one_bf, context, ((0,), (0,)))
        d_context = (
            dot(d_one_bf, w_proj, ((1,), (0,))).astype(jnp.bfloat16).reshape(rows, heads, HEAD_DIM)
        )
        scores = (
            jnp.einsum("qhd,khd->hqk", query, key, preferred_element_type=jnp.float32) * score_scale
        )
        scores = jnp.where(same_doc, scores, -1e30)
        soft = jnp.exp(scores - log_total)
        d_values = jnp.einsum(
            "hqk,qhd->khd", soft.astype(jnp.bfloat16), d_context, preferred_element_type=jnp.float32
        )
        d_probs = jnp.einsum("qhd,khd->hqk", d_context, value, preferred_element_type=jnp.float32)
        d_scores = (soft * (d_probs - jnp.sum(soft * d_probs, axis=-1, keepdims=True))).astype(
            jnp.bfloat16
        )
        d_queries = (
            jnp.einsum("hqk,khd->qhd", d_scores, key, preferred_element_type=jnp.float32)
            * score_scale
        )
        d_keys = (
            jnp.einsum("hqk,qhd->khd", d_scores, query, preferred_element_type=jnp.float32)
            * score_scale
        )
        d_qkv = jnp.concatenate(
            [
                d_queries.reshape(rows, width),
                own_rows(d_keys.reshape(seq_len, width)),
                own_rows(d_values.reshape(seq_len, width)),
            ],
            axis=1,
        ).astype(jnp.bfloat16)
        grad_bias_qkv = jnp.sum(d_qkv, axis=0, dtype=jnp.float32)
        grad_w_qkv = dot(hidden_bf, d_qkv, ((0,), (0,)))
        upstream = d_one + dot(d_qkv, w_qkv, ((1,), (1,)))
        whole = jnp.concatenate([grad_w_qkv, grad_w_proj, grad_w_in, grad_w_out], axis=1)
        pieces[layer] = lax.psum_scatter(
            whole.astype(jnp.bfloat16), BOTH, scatter_dimension=0, tiled=True
        )
        col_parts[layer] = jnp.concatenate(
            [
                grad_bias_qkv[:width][None],
                grad_bias_qkv[2 * width :][None],
                grad_bias_in.reshape(blocks, width),
            ],
            axis=0,
        )
        row_parts[layer] = jnp.stack(
            [grad_bias_proj, grad_bias_two, gain_one, shift_one, gain_two, shift_two]
        )
    small = lax.psum(jnp.stack([jnp.stack(col_parts), jnp.stack(row_parts)]), BOTH)
    row_total = small[1]
    col_total = lax.dynamic_slice_in_dim(small[0], tensor_index * col_width, col_width, axis=2)
    summed = jnp.concatenate(
        [part.reshape(piece, per_layer, width).transpose(1, 0, 2) for part in pieces], axis=0
    )
    slot_ids = jnp.arange(slots, dtype=jnp.int32)
    named = unit_slot[None, :] == slot_ids[:, None]
    holds = jnp.any(named, axis=1)
    unit_of = jnp.argmax(named, axis=1)
    back = jnp.where(holds[:, None, None], summed[unit_of], jnp.zeros((), jnp.bfloat16))
    back = back.reshape(dp_size, slot_count, piece, tensor_size, col_width)
    back = back.transpose(0, 3, 1, 2, 4).reshape(devices, slot_count, piece, col_width)
    owned = lax.all_to_all(back, BOTH, 0, 0)
    owned = owned.transpose(1, 0, 2, 3).reshape(slot_count, width, col_width).astype(jnp.float32)
    occupied = lax.dynamic_slice_in_dim(holds, lax.axis_index("dp") * slot_count, slot_count)
    occupied = occupied.astype(jnp.float32)[:, None, None]
    new_master, new_first, new_second = adamw_update(
        masters, owned, first_moment, second_moment, RATE_UNITS
    )
    unit_master = new_master * occupied
    unit_state = jnp.stack([new_first * occupied, new_second * occupied])
    new_col, col_first, col_second = adamw_update(
        column_state[0], col_total, column_state[1], column_state[2], RATE_SMALL
    )
    column_out = jnp.stack([col_total, new_col, col_first, col_second])
    new_row, row_first, row_second = adamw_update(
        row_state[0], row_total, row_state[1], row_state[2], RATE_SMALL
    )
    row_out = jnp.stack([row_total, new_row, row_first, row_second])
    return (hidden, upstream, unit_master, unit_state, column_out, row_out)


def solution(mesh):
    return jax.shard_map(
        local,
        mesh=mesh,
        in_specs=(
            P(("dp", "tensor"), None),
            P("dp", None),
            P(),
            P("dp", None, "tensor"),
            P("dp", None, "tensor"),
            P("dp", None, "tensor"),
            P(None, None, None, "tensor"),
            P(),
            P(("dp", "tensor"), None),
        ),
        out_specs=(
            P(("dp", "tensor"), None),
            P(("dp", "tensor"), None),
            P("dp", None, "tensor"),
            P(None, "dp", None, "tensor"),
            P(None, None, None, "tensor"),
            P(),
        ),
        check_vma=False,
    )
```

profile of v0, /device:TPU:8, one launch (start us, length us, event | category | flops | bytes accessed | tf_op | source)
XLA Modules:
  0.0 1338.4 jit_solution(5560922566335390330)
XLA Ops:
  11.2 6.0 all-to-all-start
  17.3 46.5 %all-to-all-done = bf16[32,4,32,256]{3,2,1,0:T(8,128)(2,1)S(1)} async-done(((bf16[32,4,32,256]{3,2,1,0:T(8,128)(2,1)}), bf16[32,4,32,256]{3,2,1,0:T(8,128)(2,1)S(1)}, u32[]{:S(2)}, u32[]{:S(2)}) %all-to-all-start) | async-done | bytes 2097184 | tf_op jit(solution)/shard_map/all_to_all | solution.py:97
  75.9 5.5 all-gather
  83.2 145.9 %all-gather.4.cloned.1.call-done = bf16[1024,12288]{1,0:T(8,128)(2,1)} async-done(((bf16[32,12288]{1,0:T(8,128)(2,1)}), bf16[1024,12288]{1,0:T(8,128)(2,1)}) %all-gather.4.cloned.1.call-update) | async-done | bytes 25165840 | tf_op jit(solution)/shard_map/all_gather | solution.py:104
  229.1 5.7 fusion.44
  235.3 7.6 fusion
  242.9 9.4 exponential_reduce_fusion.1
  252.4 8.3 convolution_convert_fusion.10
  264.6 18.3 %multiply_convert_fusion.5 = (bf16[512,4096]{1,0:T(8,128)(2,1)S(1)}, f32[512,4096]{1,0:T(8,128)}) fusion(f32[4096]{0:T(1024)S(1)} %bitcast.236, bf16[1024,12288]{1,0:T(8,128)(2,1)} %all-gather.4.cloned.1.call-done, f32[512,1024]{1,0:T(8,128)S(1)} %get-tuple-element.76, f32[1024]{0:T(1024)S(1)} %bitcast.252, f32[1024]{0:T(1024)S(1)} %bitcast.222, ...), kind=kOutput, calls=%fused_computation.40 | convolution fusion | flops 4366794752 | bytes 23097344 | tf_op jit(solution)/shard_map/dot_general | solution.py:66
  283.0 8.7 fusion.138
  292.1 93.3 %all-gather.6.cloned.1.call-done = bf16[1024,12288]{1,0:T(8,128)(2,1)} async-done(((bf16[32,12288]{1,0:T(8,128)(2,1)}), bf16[1024,12288]{1,0:T(8,128)(2,1)}) %all-gather.6.cloned.1.call-update) | async-done | bytes 25165840 | tf_op jit(solution)/shard_map/all_gather | solution.py:104
  385.4 5.8 fusion.38
  394.0 7.7 fusion.1
  401.8 9.5 exponential_reduce_fusion
  411.9 8.2 convolution_convert_fusion.9
  420.2 3.8 fusion.139
  424.4 18.3 %multiply_convert_fusion.4 = (bf16[512,4096]{1,0:T(8,128)(2,1)S(1)}, f32[512,4096]{1,0:T(8,128)}) fusion(f32[4096]{0:T(1024)S(1)} %bitcast.238, bf16[1024,12288]{1,0:T(8,128)(2,1)} %all-gather.6.cloned.1.call-done, f32[512,1024]{1,0:T(8,128)S(1)} %get-tuple-element.84, f32[1024]{0:T(1024)S(1)} %bitcast.246, f32[1024]{0:T(1024)S(1)} %bitcast.212, ...), kind=kOutput, calls=%fused_computation.39 | convolution fusion | flops 4366794752 | bytes 23097344 | tf_op jit(solution)/shard_map/dot_general | solution.py:66
  442.7 8.8 fusion.140
  456.2 19.0 %convert_reduce_fusion = (f32[4096]{0:T(1024)}, bf16[512,4096]{1,0:T(8,128)(2,1)S(1)}) fusion(f32[512,4096]{1,0:T(8,128)} %get-tuple-element.86, f32[4096]{0:T(1024)S(1)} %bitcast.239, bf16[1024,12288]{1,0:T(8,128)(2,1)} %all-gather.6.cloned.1.call-done, f32[512,1024]{1,0:T(8,128)S(1)} %get-tuple-element.36), kind=kOutput, calls=%fused_computation.35 | convolution fusion | flops 4379373568 | bytes 23101440 | tf_op jit(solution)/shard_map/dot_general | solution.py:66
  475.2 9.7 multiply_reduce_fusion.2
  491.0 11.8 multiply_reduce_fusion.1
  502.8 12.6 multiply_convert_fusion.1
  519.6 8.4 convolution_convert_fusion.8
  528.1 8.0 multiply_reduce_fusion.3
  537.5 19.3 %convert_reduce_fusion.1 = (f32[4096]{0:T(1024)}, bf16[512,4096]{1,0:T(8,128)(2,1)S(1)}) fusion(f32[512,4096]{1,0:T(8,128)} %get-tuple-element.78, f32[4096]{0:T(1024)S(1)} %bitcast.237, bf16[1024,12288]{1,0:T(8,128)(2,1)} %all-gather.4.cloned.1.call-done, f32[512,1024]{1,0:T(8,128)S(1)} %get-tuple-element.32), kind=kOutput, calls=%fused_computation.36 | convolution fusion | flops 4379373568 | bytes 23101440 | tf_op jit(solution)/shard_map/dot_general | solution.py:66
  556.8 9.1 multiply_reduce_fusion.4
  568.0 3.9 fusion.86
  573.4 12.1 multiply_reduce_fusion
  585.5 12.6 multiply_convert_fusion
  602.3 8.4 convolution_convert_fusion.7
  610.8 7.4 convolution_convert_fusion.3
  618.2 6.9 convolution_convert_fusion.2
  627.6 9.4 convert_bitcast_fusion
  637.0 8.6 copy.144
  648.5 16.8 %pad_maximum_fusion = bf16[1024,12288]{1,0:T(8,128)(2,1)} fusion(bf16[1024,4096]{1,0:T(8,128)(2,1)} %convolution_convert_fusion.2, bf16[1024,4096]{1,0:T(8,128)(2,1)} %convolution_convert_fusion.3, bf16[1024,1024]{1,0:T(8,128)(2,1)S(1)} %copy.145, bf16[1024,3072]{1,0:T(8,128)(2,1)} %copy.144), kind=kLoop, calls=%fused_computation.2 | loop fusion | flops 100663296 | bytes 50331648 | tf_op jit(solution)/shard_map/concatenate | solution.py:239
  665.4 4.6 convolution_convert_fusion.5
  670.0 3.9 copy.147
  674.0 8.6 convolution_convert_fusion.4
  682.6 6.9 convolution_convert_fusion
  689.6 7.4 convolution_convert_fusion.1
  697.0 19.4 %pad_maximum_fusion.1 = bf16[1024,12288]{1,0:T(8,128)(2,1)} fusion(bf16[1024,4096]{1,0:T(8,128)(2,1)} %convolution_convert_fusion, bf16[1024,4096]{1,0:T(8,128)(2,1)} %convolution_convert_fusion.1, bf16[1024,1024]{1,0:T(8,128)(2,1)S(1)} %copy-done.19, bf16[1024,3072]{1,0:T(8,128)(2,1)} %convolution_convert_fusion.4), kind=kLoop, calls=%fused_computation.3 | loop fusion | flops 100663296 | bytes 50331648 | tf_op jit(solution)/shard_map/concatenate | solution.py:239
  717.9 193.0 %reduce-scatter.3.cloned.1.call-done = bf16[32,12288]{1,0:T(8,128)(2,1)} async-done(((bf16[1024,12288]{1,0:T(8,128)(2,1)}), bf16[32,12288]{1,0:T(8,128)(2,1)}) %reduce-scatter.3.cloned.1.call-update) | async-done | bytes 786448 | tf_op jit(solution)/shard_map/reduce_scatter | solution.py:240
  913.0 250.4 %reduce-scatter.5.cloned.1.call-done = bf16[32,12288]{1,0:T(8,128)(2,1)} async-done(((bf16[1024,12288]{1,0:T(8,128)(2,1)}), bf16[32,12288]{1,0:T(8,128)(2,1)}) %reduce-scatter.5.cloned.1.call-update) | async-done | bytes 786448 | tf_op jit(solution)/shard_map/reduce_scatter | solution.py:240
  1172.9 4.5 all-to-all-start.1
  1183.6 9.2 fusion.80
  1192.8 122.3 %all-reduce.2.cloned.1.call-done = f32[2,2,6,1024]{3,1,2,0:T(2,128)} async-done(((f32[2,2,6,1024]{3,1,2,0:T(2,128)}), f32[2,2,6,1024]{3,1,2,0:T(2,128)}) %all-reduce.2.cloned.1.call-update) | async-done | bytes 98320 | tf_op jit(solution)/shard_map/psum | solution.py:254
  1322.4 5.2 multiply_bitcast_fusion.1
  1327.6 4.0 pad_maximum_fusion.2
  (310 shorter events, 81.7 us)
Async XLA Ops:
  7.2 74.2 %copy-start = (s32[4,512]{1,0:T(4,128)S(1)}, s32[4,512]{1,0:T(4,128)}, u32[]{:S(2)}) copy-start(s32[4,512]{1,0:T(4,128)} %param.10) | copy-start | bytes 24580
  7.2 10.1 copy-start.89
  11.2 52.7 %all-to-all-start = ((bf16[32,4,32,256]{3,2,1,0:T(8,128)(2,1)}), bf16[32,4,32,256]{3,2,1,0:T(8,128)(2,1)S(1)}, u32[]{:S(2)}, u32[]{:S(2)}) async-start(bf16[32,4,32,256]{3,2,1,0:T(8,128)(2,1)} %copy.127), calls=%async_computation | async-start | bytes 4194304 | tf_op jit(solution)/shard_map/all_to_all | solution.py:97
  17.2 211.9 %all-gather.4.cloned.1.call-start = ((), (), s32[]{:S(2)}) async-start(), calls=%async_computation.4 | async-start | bytes 25952256 | tf_op jit(solution)/shard_map/all_gather | solution.py:104
  72.2 156.9 %copy-start.86 = (bf16[512,1024]{1,0:T(8,128)(2,1)S(1)}, bf16[512,1024]{1,0:T(8,128)(2,1)}, u32[]{:S(2)}) copy-start(bf16[512,1024]{1,0:T(8,128)(2,1)} %param.9) | copy-start | bytes 3145732
  74.8 310.6 %all-gather.6.cloned.1.call-start = ((), (), s32[]{:S(2)}) async-start(), calls=%async_computation.5 | async-start | bytes 25952256 | tf_op jit(solution)/shard_map/all_gather | solution.py:104
  75.8 835.1 %reduce-scatter.3.cloned.1.call-start = ((), (), s32[]{:S(2)}) async-start(), calls=%async_computation.6 | async-start | bytes 25952256 | tf_op jit(solution)/shard_map/reduce_scatter | solution.py:240
  82.9 200.0 %copy-start.62 = (f32[1,1,1,1024]{3,1,2,0:T(1,128)}, f32[1,1,1,1024]{3,1,2,0:T(1,128)S(1)}, u32[]{:S(2)}) copy-start(f32[1,1,1,1024]{3,1,2,0:T(1,128)S(1)} %get-tuple-element.58) | copy-start | bytes 12292
  82.9 200.0 %copy-start.84 = (f32[1,1,1,1024]{3,1,2,0:T(1,128)}, f32[1,1,1,1024]{3,1,2,0:T(1,128)S(1)}, u32[]{:S(2)}) copy-start(f32[1,1,1,1024]{3,1,2,0:T(1,128)S(1)} %get-tuple-element.57) | copy-start | bytes 12292
  82.9 337.2 %copy-start.59 = (f32[1,1,1,1024]{3,1,2,0:T(1,128)}, f32[1,1,1,1024]{3,1,2,0:T(1,128)S(1)}, u32[]{:S(2)}) copy-start(f32[1,1,1,1024]{3,1,2,0:T(1,128)S(1)} %get-tuple-element.55) | copy-start | bytes 12292
  82.9 337.2 %copy-start.82 = (f32[1,1,1,1024]{3,1,2,0:T(1,128)}, f32[1,1,1,1024]{3,1,2,0:T(1,128)S(1)}, u32[]{:S(2)}) copy-start(f32[1,1,1,1024]{3,1,2,0:T(1,128)S(1)} %get-tuple-element.54) | copy-start | bytes 12292
  82.9 359.8 %copy-start.80 = (f32[1,1,1,1024]{3,1,2,0:T(1,128)}, f32[1,1,1,1024]{3,1,2,0:T(1,128)S(1)}, u32[]{:S(2)}) copy-start(f32[1,1,1,1024]{3,1,2,0:T(1,128)S(1)} %get-tuple-element.51) | copy-start | bytes 12292
  83.0 402.0 %copy-start.57 = (f32[1,1,1,1024]{3,1,2,0:T(1,128)}, f32[1,1,1,1024]{3,1,2,0:T(1,128)S(1)}, u32[]{:S(2)}) copy-start(f32[1,1,1,1024]{3,1,2,0:T(1,128)S(1)} %get-tuple-element.52) | copy-start | bytes 12292
  83.0 181.6 %copy-start.67 = (f32[1,4,1024]{2,0,1:T(1,128)}, f32[1,4,1024]{2,0,1:T(1,128)S(1)}, u32[]{:S(2)}) copy-start(f32[1,4,1024]{2,0,1:T(1,128)S(1)} %get-tuple-element.64) | copy-start | bytes 49156
  235.3 17.1 %copy-start.26 = (bf16[512,1024]{0,1:T(8,128)(2,1)}, bf16[512,1024]{0,1:T(8,128)(2,1)S(1)}, u32[]{:S(2)}) copy-start(bf16[512,1024]{0,1:T(8,128)(2,1)S(1)} %get-tuple-element.45) | copy-start | bytes 3145732
  264.2 18.8 %copy-start.15 = (f32[512,1024]{1,0:T(8,128)}, f32[512,1024]{1,0:T(8,128)S(1)}, u32[]{:S(2)}) copy-start(f32[512,1024]{1,0:T(8,128)S(1)} %get-tuple-element.76) | copy-start | bytes 6291460
  264.2 18.7 %copy-start.48 = (f32[512]{0:T(512)}, f32[512]{0:T(512)S(1)}, u32[]{:S(2)}) copy-start(f32[512]{0:T(512)S(1)} %broadcast_multiply_fusion.11) | copy-start | bytes 6148
  264.6 18.4 %copy-start.72 = (f32[512]{0:T(512)}, f32[512]{0:T(512)S(1)}, u32[]{:S(2)}) copy-start(f32[512]{0:T(512)S(1)} %add_rsqrt_fusion.3) | copy-start | bytes 6148
  291.7 99.5 %copy-start.11 = (f32[512,1024]{1,0:T(8,128)}, f32[512,1024]{1,0:T(8,128)S(1)}, u32[]{:S(2)}) copy-start(f32[512,1024]{1,0:T(8,128)S(1)} %get-tuple-element.80) | copy-start | bytes 6291460
  291.7 128.4 %copy-start.45 = (f32[512]{0:T(512)}, f32[512]{0:T(512)S(1)}, u32[]{:S(2)}) copy-start(f32[512]{0:T(512)S(1)} %broadcast_multiply_fusion.10) | copy-start | bytes 6148
  292.1 128.1 %copy-start.69 = (f32[512]{0:T(512)}, f32[512]{0:T(512)S(1)}, u32[]{:S(2)}) copy-start(f32[512]{0:T(512)S(1)} %add_rsqrt_fusion.2) | copy-start | bytes 6148
  424.0 60.9 %copy-start.17 = (f32[512,1024]{1,0:T(8,128)}, f32[512,1024]{1,0:T(8,128)S(1)}, u32[]{:S(2)}) copy-start(f32[512,1024]{1,0:T(8,128)S(1)} %get-tuple-element.84) | copy-start | bytes 6291460
  424.0 60.9 %copy-start.50 = (f32[512]{0:T(512)}, f32[512]{0:T(512)S(1)}, u32[]{:S(2)}) copy-start(f32[512]{0:T(512)S(1)} %broadcast_multiply_fusion.9) | copy-start | bytes 6148
  424.4 60.6 %copy-start.74 = (f32[512]{0:T(512)}, f32[512]{0:T(512)S(1)}, u32[]{:S(2)}) copy-start(f32[512]{0:T(512)S(1)} %add_rsqrt_fusion.1) | copy-start | bytes 6148
  442.7 10.7 copy-start.64
  456.2 19.0 %copy-start.32 = (f32[512,1024]{1,0:T(8,128)}, f32[512,1024]{1,0:T(8,128)S(1)}, u32[]{:S(2)}) copy-start(f32[512,1024]{1,0:T(8,128)S(1)} %get-tuple-element.36) | copy-start | bytes 6291460
  475.2 9.7 copy-start.98
  502.8 12.6 copy-start.6
  516.9 11.1 copy-start.20
  537.4 19.4 %copy-start.36 = (f32[512,1024]{1,0:T(8,128)}, f32[512,1024]{1,0:T(8,128)S(1)}, u32[]{:S(2)}) copy-start(f32[512,1024]{1,0:T(8,128)S(1)} %get-tuple-element.32) | copy-start | bytes 6291460
  537.4 19.4 %copy-start.16 = (f32[512,1024]{1,0:T(8,128)S(1)}, f32[512,1024]{1,0:T(8,128)}, u32[]{:S(2)}) copy-start(f32[512,1024]{1,0:T(8,128)} %copy-done.15) | copy-start | bytes 6291460
  537.4 19.4 %copy-start.49 = (f32[512]{0:T(512)S(1)}, f32[512]{0:T(512)}, u32[]{:S(2)}) copy-start(f32[512]{0:T(512)} %copy-done.48) | copy-start | bytes 6148
  537.4 19.4 %copy-start.63 = (f32[1,1,1,1024]{3,1,2,0:T(1,128)S(1)}, f32[1,1,1,1024]{3,1,2,0:T(1,128)}, u32[]{:S(2)}) copy-start(f32[1,1,1,1024]{3,1,2,0:T(1,128)} %copy-done.62) | copy-start | bytes 12292
  537.4 19.4 %copy-start.73 = (f32[512]{0:T(512)S(1)}, f32[512]{0:T(512)}, u32[]{:S(2)}) copy-start(f32[512]{0:T(512)} %copy-done.72) | copy-start | bytes 6148
  585.5 12.6 copy-start.4
  599.7 27.9 %copy-start.22 = (bf16[16,64,512]{2,1,0:T(8,128)(2,1)}, bf16[16,64,512]{2,1,0:T(8,128)(2,1)S(1)}, u32[]{:S(2)}) copy-start(bf16[16,64,512]{2,1,0:T(8,128)(2,1)S(1)} %multiply_convert_fusion.7) | copy-start | bytes 3145732
  602.3 25.3 %copy-start.25 = (bf16[16,64,512]{2,1,0:T(8,128)(2,1)}, bf16[16,64,512]{2,1,0:T(8,128)(2,1)S(1)}, u32[]{:S(2)}) copy-start(bf16[16,64,512]{2,1,0:T(8,128)(2,1)S(1)} %multiply_convert_fusion.6) | copy-start | bytes 3145732
  610.8 16.9 %copy-start.39 = (bf16[16,64,512]{2,1,0:T(8,128)(2,1)}, bf16[16,64,512]{2,1,0:T(8,128)(2,1)S(1)}, u32[]{:S(2)}) copy-start(bf16[16,64,512]{2,1,0:T(8,128)(2,1)S(1)} %convolution_convert_fusion.7) | copy-start | bytes 3145732
  665.4 498.1 %reduce-scatter.5.cloned.1.call-start = ((), (), s32[]{:S(2)}) async-start(), calls=%async_computation.7 | async-start | bytes 25952256 | tf_op jit(solution)/shard_map/reduce_scatter | solution.py:240
  1172.9 9.7 copy-start.53
  1172.9 9.7 copy-start.54
  1172.9 9.7 copy-start.55
  1172.9 9.7 copy-start.76
  1172.9 9.7 copy-start.77
  1172.9 144.7 %all-to-all-start.1 = ((bf16[32,4,32,256]{3,2,1,0:T(8,128)(2,1)}), bf16[32,4,32,256]{3,2,1,0:T(8,128)(2,1)S(1)}, u32[]{:S(2)}, u32[]{:S(2)}) async-start(bf16[32,4,32,256]{3,2,1,0:T(8,128)(2,1)} %bitcast.167), calls=%async_computation.3 | async-start | bytes 4194304 | tf_op jit(solution)/shard_map/all_to_all | solution.py:267
  1177.4 137.7 %all-reduce.2.cloned.1.call-start = ((), (), s32[]{:S(2)}) async-start(), calls=%async_computation.8 | async-start | bytes 196608 | tf_op jit(solution)/shard_map/psum | solution.py:254
  1183.6 131.6 %copy-start.42 = (f32[3,2,6,1024]{3,1,2,0:T(2,128)S(1)}, f32[3,2,6,1024]{3,1,2,0:T(2,128)}, u32[]{:S(2)}) copy-start(f32[3,2,6,1024]{3,1,2,0:T(2,128)} %param.16) | copy-start | bytes 442372
  1183.6 132.5 %copy-start.43 = (f32[3,2,6,256]{3,1,2,0:T(2,128)S(1)}, f32[3,2,6,256]{3,1,2,0:T(2,128)}, u32[]{:S(2)}) copy-start(f32[3,2,6,256]{3,1,2,0:T(2,128)} %param.15) | copy-start | bytes 110596
  (62 other events, 434.5 us)
Sparse Core Ops, SparseCore 0:
  74.9 154.1 all-gather.3
  232.6 152.7 all-gather.5
  665.4 245.4 reduce-scatter.2
  918.4 245.0 reduce-scatter.4
  1184.1 130.9 all-reduce.1
where the time goes:
time: 1340 us
  waiting for transfers between devices  852 us (64%)
  matrix products  289 us (22%)
  other arithmetic  115 us (9%)
  local copies, waits for them, and re-layouts  51.2 us (4%)
  between operations  15.6 us (1%)
    reduce_scatter x2, waiting for transfers between devices, local(): lax.psum_scatter(whole.astype(jnp.bfloat16), BOTH, scatter_dimension=0, t...  443 us
    all_gather x2, waiting for transfers between devices, local(): lax.all_gather(own.reshape(piece, per_layer * width), BOTH, axis=0, tiled...  239 us
    dot_general x24, matrix products, dot(): lax.dot_general(left, right, (dims, ((), ())), preferred_element_type=jnp...  208 us
    psum x1, waiting for transfers between devices, local(): lax.psum(jnp.stack([jnp.stack(col_parts), jnp.stack(row_parts)]), BOTH)  122 us
    all_to_all x1, waiting for transfers between devices, local(): spread = lax.all_to_all(sent.transpose(1, 0, 2, 3), BOTH, 0, 0)  46.5 us
    concatenate x2, other arithmetic, local(): jnp.concatenate([grad_w_qkv, grad_w_proj, grad_w_in, grad_w_out], axis=1)  36.2 us
  transfers between devices with their start and end apart: 7, of which 6 were waited for; matrix products, arithmetic and copies ran while one was open for 10% of the time, Pallas kernels for 0%

commit v1 on v0

--- a/solution.py
+++ b/solution.py
@@ -251,7 +251,9 @@
         row_parts[layer] = jnp.stack(
             [grad_bias_proj, grad_bias_two, gain_one, shift_one, gain_two, shift_two]
         )
-    small = lax.psum(jnp.stack([jnp.stack(col_parts), jnp.stack(row_parts)]), BOTH)
+    small = jnp.sum(
+        lax.all_gather(jnp.stack([jnp.stack(col_parts), jnp.stack(row_parts)]), BOTH), axis=0
+    )
     row_total = small[1]
     col_total = lax.dynamic_slice_in_dim(small[0], tensor_index * col_width, col_width, axis=2)
     summed = jnp.concatenate(

time: 1340 us -> 1270 us (0.948)
  waiting for transfers between devices: 852 us -> 772 us
    psum x1 -> x0, waiting for transfers between devices: 122 us -> none  [local(): lax.psum(jnp.stack([jnp.stack(col_parts), jnp.stack(row_parts)]), BOTH)]
    all_gather x0 -> x1, waiting for transfers between devices: none -> 48.7 us  [local(): lax.all_gather(jnp.stack([jnp.stack(col_parts), jnp.stack(row_parts)]), B...]
  transfers between devices with their start and end apart: 7 -> 7, of which waited for: 6 -> 6; matrix products, arithmetic and copies ran while one was open for 10% -> 12% of each run, Pallas kernels for 0% -> 0%
where the time goes in v1:
time: 1270 us; the launch traced here: 1260 us
  waiting for transfers between devices  772 us (61%)
  matrix products  288 us (23%)
  other arithmetic  116 us (9%)
  local copies, waits for them, and re-layouts  50.8 us (4%)
  between operations  15.7 us (1%)
    reduce_scatter x2, waiting for transfers between devices, local(): lax.psum_scatter(whole.astype(jnp.bfloat16), BOTH, scatter_dimension=0, t...  438 us
    all_gather x2, waiting for transfers between devices, local(): lax.all_gather(own.reshape(piece, per_layer * width), BOTH, axis=0, tiled...  239 us
    dot_general x24, matrix products, dot(): lax.dot_general(left, right, (dims, ((), ())), preferred_element_type=jnp...  207 us
    all_gather x1, waiting for transfers between devices, local(): lax.all_gather(jnp.stack([jnp.stack(col_parts), jnp.stack(row_parts)]), B...  48.7 us
    all_to_all x1, waiting for transfers between devices, local(): spread = lax.all_to_all(sent.transpose(1, 0, 2, 3), BOTH, 0, 0)  46.5 us
    concatenate x2, other arithmetic, local(): jnp.concatenate([grad_w_qkv, grad_w_proj, grad_w_in, grad_w_out], axis=1)  36.1 us
  transfers between devices with their start and end apart: 7, of which 6 were waited for; matrix products, arithmetic and copies ran while one was open for 12% of the time, Pallas kernels for 0%

profile of v1, /device:TPU:8, one launch (start us, length us, event | category | flops | bytes accessed | tf_op | source)
XLA Modules:
  0.0 1258.8 jit_solution(1376501526680302810)
XLA Ops:
  11.2 6.0 all-to-all-start
  17.3 46.5 %all-to-all-done = bf16[32,4,32,256]{3,2,1,0:T(8,128)(2,1)S(1)} async-done(((bf16[32,4,32,256]{3,2,1,0:T(8,128)(2,1)}), bf16[32,4,32,256]{3,2,1,0:T(8,128)(2,1)S(1)}, u32[]{:S(2)}, u32[]{:S(2)}) %all-to-all-start) | async-done | bytes 2097184 | tf_op jit(solution)/shard_map/all_to_all | solution.py:97
  75.9 5.5 all-gather
  83.2 145.9 %all-gather.6.cloned.1.call-done = bf16[1024,12288]{1,0:T(8,128)(2,1)} async-done(((bf16[32,12288]{1,0:T(8,128)(2,1)}), bf16[1024,12288]{1,0:T(8,128)(2,1)}) %all-gather.6.cloned.1.call-update) | async-done | bytes 25165840 | tf_op jit(solution)/shard_map/all_gather | solution.py:104
  229.1 5.6 fusion.44
  235.3 7.6 fusion
  242.9 9.4 exponential_reduce_fusion.1
  252.4 8.3 convolution_convert_fusion.10
  264.6 18.3 %multiply_convert_fusion.5 = (bf16[512,4096]{1,0:T(8,128)(2,1)S(1)}, f32[512,4096]{1,0:T(8,128)}) fusion(f32[4096]{0:T(1024)S(1)} %bitcast.238, bf16[1024,12288]{1,0:T(8,128)(2,1)} %all-gather.6.cloned.1.call-done, f32[512,1024]{1,0:T(8,128)S(1)} %get-tuple-element.76, f32[1024]{0:T(1024)S(1)} %bitcast.254, f32[1024]{0:T(1024)S(1)} %bitcast.224, ...), kind=kOutput, calls=%fused_computation.40 | convolution fusion | flops 4366794752 | bytes 23097344 | tf_op jit(solution)/shard_map/dot_general | solution.py:66
  283.0 8.7 fusion.138
  292.1 93.3 %all-gather.8.cloned.1.call-done = bf16[1024,12288]{1,0:T(8,128)(2,1)} async-done(((bf16[32,12288]{1,0:T(8,128)(2,1)}), bf16[1024,12288]{1,0:T(8,128)(2,1)}) %all-gather.8.cloned.1.call-update) | async-done | bytes 25165840 | tf_op jit(solution)/shard_map/all_gather | solution.py:104
  385.4 5.8 fusion.38
  394.0 7.7 fusion.1
  401.8 9.5 exponential_reduce_fusion
  411.9 8.2 convolution_convert_fusion.9
  420.2 3.8 fusion.139
  424.4 18.3 %multiply_convert_fusion.4 = (bf16[512,4096]{1,0:T(8,128)(2,1)S(1)}, f32[512,4096]{1,0:T(8,128)}) fusion(f32[4096]{0:T(1024)S(1)} %bitcast.240, bf16[1024,12288]{1,0:T(8,128)(2,1)} %all-gather.8.cloned.1.call-done, f32[512,1024]{1,0:T(8,128)S(1)} %get-tuple-element.84, f32[1024]{0:T(1024)S(1)} %bitcast.248, f32[1024]{0:T(1024)S(1)} %bitcast.214, ...), kind=kOutput, calls=%fused_computation.39 | convolution fusion | flops 4366794752 | bytes 23097344 | tf_op jit(solution)/shard_map/dot_general | solution.py:66
  442.8 8.8 fusion.140
  456.2 19.0 %convert_reduce_fusion = (f32[4096]{0:T(1024)}, bf16[512,4096]{1,0:T(8,128)(2,1)S(1)}) fusion(f32[512,4096]{1,0:T(8,128)} %get-tuple-element.86, f32[4096]{0:T(1024)S(1)} %bitcast.241, bf16[1024,12288]{1,0:T(8,128)(2,1)} %all-gather.8.cloned.1.call-done, f32[512,1024]{1,0:T(8,128)S(1)} %get-tuple-element.36), kind=kOutput, calls=%fused_computation.35 | convolution fusion | flops 4379373568 | bytes 23101440 | tf_op jit(solution)/shard_map/dot_general | solution.py:66
  475.2 9.7 multiply_reduce_fusion.2
  491.0 11.8 multiply_reduce_fusion.1
  502.8 12.6 multiply_convert_fusion.1
  519.6 8.4 convolution_convert_fusion.8
  528.1 8.0 multiply_reduce_fusion.3
  537.4 18.7 %convert_reduce_fusion.1 = (f32[4096]{0:T(1024)S(1)}, bf16[512,4096]{1,0:T(8,128)(2,1)S(1)}) fusion(f32[512,4096]{1,0:T(8,128)} %get-tuple-element.78, f32[4096]{0:T(1024)S(1)} %bitcast.239, bf16[1024,12288]{1,0:T(8,128)(2,1)} %all-gather.6.cloned.1.call-done, f32[512,1024]{1,0:T(8,128)S(1)} %get-tuple-element.32), kind=kOutput, calls=%fused_computation.36 | convolution fusion | flops 4379373568 | bytes 23101440 | tf_op jit(solution)/shard_map/dot_general | solution.py:66
  556.3 9.1 multiply_reduce_fusion.4
  567.4 3.8 fusion.86
  572.8 12.4 multiply_reduce_fusion
  585.1 12.6 %multiply_convert_fusion = bf16[16,512,512]{1,2,0:T(8,128)(2,1)S(1)} fusion(f32[16,512,512]{1,2,0:T(8,128)} %get-tuple-element.95, f32[16,512,512]{1,2,0:T(8,128)} %get-tuple-element.74, f32[16,512]{1,0:T(8,128)S(1)} %get-tuple-element.94, f32[16,512]{1,0:T(8,128)S(1)} %copy-done.43, pred[512,512]{0,1:T(8,128)(4,1)S(1)} %broadcast_compare_fusion), kind=kLoop, calls=%fused_computation.4 | loop fusion | flops 25165824 | bytes 42270720 | tf_op jit(solution)/shard_map/convert_element_type | solution.py:217
  602.0 8.4 convolution_convert_fusion.7
  610.4 7.3 convolution_convert_fusion.3
  617.7 6.9 convolution_convert_fusion.2
  627.1 9.4 convert_bitcast_fusion
  636.5 8.6 copy.144
  648.0 16.8 %pad_maximum_fusion = bf16[1024,12288]{1,0:T(8,128)(2,1)} fusion(bf16[1024,4096]{1,0:T(8,128)(2,1)} %convolution_convert_fusion.2, bf16[1024,4096]{1,0:T(8,128)(2,1)} %convolution_convert_fusion.3, bf16[1024,1024]{1,0:T(8,128)(2,1)S(1)} %copy.145, bf16[1024,3072]{1,0:T(8,128)(2,1)} %copy.144), kind=kLoop, calls=%fused_computation.2 | loop fusion | flops 100663296 | bytes 50331648 | tf_op jit(solution)/shard_map/concatenate | solution.py:239
  664.9 4.6 convolution_convert_fusion.5
  669.5 3.9 copy.147
  673.5 9.1 convolution_convert_fusion.4
  682.6 6.9 convolution_convert_fusion
  689.5 7.3 convolution_convert_fusion.1
  696.9 19.3 %pad_maximum_fusion.1 = bf16[1024,12288]{1,0:T(8,128)(2,1)} fusion(bf16[1024,4096]{1,0:T(8,128)(2,1)} %convolution_convert_fusion, bf16[1024,4096]{1,0:T(8,128)(2,1)} %convolution_convert_fusion.1, bf16[1024,1024]{1,0:T(8,128)(2,1)S(1)} %copy-done.19, bf16[1024,3072]{1,0:T(8,128)(2,1)} %convolution_convert_fusion.4), kind=kLoop, calls=%fused_computation.3 | loop fusion | flops 100663296 | bytes 50331648 | tf_op jit(solution)/shard_map/concatenate | solution.py:239
  724.0 186.4 %reduce-scatter.3.cloned.1.call-done = bf16[32,12288]{1,0:T(8,128)(2,1)} async-done(((bf16[1024,12288]{1,0:T(8,128)(2,1)}), bf16[32,12288]{1,0:T(8,128)(2,1)}) %reduce-scatter.3.cloned.1.call-update) | async-done | bytes 786448 | tf_op jit(solution)/shard_map/reduce_scatter | solution.py:240
  911.6 251.3 %reduce-scatter.5.cloned.1.call-done = bf16[32,12288]{1,0:T(8,128)(2,1)} async-done(((bf16[1024,12288]{1,0:T(8,128)(2,1)}), bf16[32,12288]{1,0:T(8,128)(2,1)}) %reduce-scatter.5.cloned.1.call-update) | async-done | bytes 786448 | tf_op jit(solution)/shard_map/reduce_scatter | solution.py:240
  1171.2 4.5 all-to-all-start.1
  1175.7 8.8 fusion.80
  1184.6 48.7 %all-gather.10.cloned.1.call-done = f32[64,2,6,1024]{3,1,2,0:T(2,128)} async-done(((f32[2,2,6,1024]{3,1,2,0:T(2,128)}), f32[64,2,6,1024]{3,1,2,0:T(2,128)}) %all-gather.10.cloned.1.call-update) | async-done | bytes 3145744 | tf_op jit(solution)/shard_map/all_gather | solution.py:255
  1242.8 5.2 multiply_bitcast_fusion.1
  1248.1 4.0 pad_maximum_fusion.2
  (313 shorter events, 82.0 us)
Async XLA Ops:
  7.2 74.2 %copy-start = (s32[4,512]{1,0:T(4,128)S(1)}, s32[4,512]{1,0:T(4,128)}, u32[]{:S(2)}) copy-start(s32[4,512]{1,0:T(4,128)} %param.10) | copy-start | bytes 24580
  7.2 10.1 copy-start.90
  11.2 52.7 %all-to-all-start = ((bf16[32,4,32,256]{3,2,1,0:T(8,128)(2,1)}), bf16[32,4,32,256]{3,2,1,0:T(8,128)(2,1)S(1)}, u32[]{:S(2)}, u32[]{:S(2)}) async-start(bf16[32,4,32,256]{3,2,1,0:T(8,128)(2,1)} %copy.127), calls=%async_computation | async-start | bytes 4194304 | tf_op jit(solution)/shard_map/all_to_all | solution.py:97
  17.2 211.9 %all-gather.6.cloned.1.call-start = ((), (), s32[]{:S(2)}) async-start(), calls=%async_computation.4 | async-start | bytes 25952256 | tf_op jit(solution)/shard_map/all_gather | solution.py:104
  72.2 156.9 %copy-start.87 = (bf16[512,1024]{1,0:T(8,128)(2,1)S(1)}, bf16[512,1024]{1,0:T(8,128)(2,1)}, u32[]{:S(2)}) copy-start(bf16[512,1024]{1,0:T(8,128)(2,1)} %param.9) | copy-start | bytes 3145732
  74.8 310.6 %all-gather.8.cloned.1.call-start = ((), (), s32[]{:S(2)}) async-start(), calls=%async_computation.5 | async-start | bytes 25952256 | tf_op jit(solution)/shard_map/all_gather | solution.py:104
  75.8 834.6 %reduce-scatter.3.cloned.1.call-start = ((), (), s32[]{:S(2)}) async-start(), calls=%async_computation.6 | async-start | bytes 25952256 | tf_op jit(solution)/shard_map/reduce_scatter | solution.py:240
  82.9 200.0 %copy-start.64 = (f32[1,1,1,1024]{3,1,2,0:T(1,128)}, f32[1,1,1,1024]{3,1,2,0:T(1,128)S(1)}, u32[]{:S(2)}) copy-start(f32[1,1,1,1024]{3,1,2,0:T(1,128)S(1)} %get-tuple-element.58) | copy-start | bytes 12292
  82.9 200.0 %copy-start.85 = (f32[1,1,1,1024]{3,1,2,0:T(1,128)}, f32[1,1,1,1024]{3,1,2,0:T(1,128)S(1)}, u32[]{:S(2)}) copy-start(f32[1,1,1,1024]{3,1,2,0:T(1,128)S(1)} %get-tuple-element.57) | copy-start | bytes 12292
  82.9 337.2 %copy-start.61 = (f32[1,1,1,1024]{3,1,2,0:T(1,128)}, f32[1,1,1,1024]{3,1,2,0:T(1,128)S(1)}, u32[]{:S(2)}) copy-start(f32[1,1,1,1024]{3,1,2,0:T(1,128)S(1)} %get-tuple-element.55) | copy-start | bytes 12292
  82.9 337.2 %copy-start.83 = (f32[1,1,1,1024]{3,1,2,0:T(1,128)}, f32[1,1,1,1024]{3,1,2,0:T(1,128)S(1)}, u32[]{:S(2)}) copy-start(f32[1,1,1,1024]{3,1,2,0:T(1,128)S(1)} %get-tuple-element.54) | copy-start | bytes 12292
  82.9 359.8 %copy-start.81 = (f32[1,1,1,1024]{3,1,2,0:T(1,128)}, f32[1,1,1,1024]{3,1,2,0:T(1,128)S(1)}, u32[]{:S(2)}) copy-start(f32[1,1,1,1024]{3,1,2,0:T(1,128)S(1)} %get-tuple-element.51) | copy-start | bytes 12292
  83.0 402.0 %copy-start.59 = (f32[1,1,1,1024]{3,1,2,0:T(1,128)}, f32[1,1,1,1024]{3,1,2,0:T(1,128)S(1)}, u32[]{:S(2)}) copy-start(f32[1,1,1,1024]{3,1,2,0:T(1,128)S(1)} %get-tuple-element.52) | copy-start | bytes 12292
  83.0 181.6 %copy-start.68 = (f32[1,4,1024]{2,0,1:T(1,128)}, f32[1,4,1024]{2,0,1:T(1,128)S(1)}, u32[]{:S(2)}) copy-start(f32[1,4,1024]{2,0,1:T(1,128)S(1)} %get-tuple-element.64) | copy-start | bytes 49156
  235.3 17.1 %copy-start.28 = (bf16[512,1024]{0,1:T(8,128)(2,1)}, bf16[512,1024]{0,1:T(8,128)(2,1)S(1)}, u32[]{:S(2)}) copy-start(bf16[512,1024]{0,1:T(8,128)(2,1)S(1)} %get-tuple-element.45) | copy-start | bytes 3145732
  264.2 18.8 %copy-start.15 = (f32[512,1024]{1,0:T(8,128)}, f32[512,1024]{1,0:T(8,128)S(1)}, u32[]{:S(2)}) copy-start(f32[512,1024]{1,0:T(8,128)S(1)} %get-tuple-element.76) | copy-start | bytes 6291460
  264.2 18.7 %copy-start.50 = (f32[512]{0:T(512)}, f32[512]{0:T(512)S(1)}, u32[]{:S(2)}) copy-start(f32[512]{0:T(512)S(1)} %broadcast_multiply_fusion.11) | copy-start | bytes 6148
  264.6 18.4 %copy-start.73 = (f32[512]{0:T(512)}, f32[512]{0:T(512)S(1)}, u32[]{:S(2)}) copy-start(f32[512]{0:T(512)S(1)} %add_rsqrt_fusion.3) | copy-start | bytes 6148
  291.7 99.5 %copy-start.11 = (f32[512,1024]{1,0:T(8,128)}, f32[512,1024]{1,0:T(8,128)S(1)}, u32[]{:S(2)}) copy-start(f32[512,1024]{1,0:T(8,128)S(1)} %get-tuple-element.80) | copy-start | bytes 6291460
  291.7 128.4 %copy-start.47 = (f32[512]{0:T(512)}, f32[512]{0:T(512)S(1)}, u32[]{:S(2)}) copy-start(f32[512]{0:T(512)S(1)} %broadcast_multiply_fusion.10) | copy-start | bytes 6148
  292.1 128.1 %copy-start.70 = (f32[512]{0:T(512)}, f32[512]{0:T(512)S(1)}, u32[]{:S(2)}) copy-start(f32[512]{0:T(512)S(1)} %add_rsqrt_fusion.2) | copy-start | bytes 6148
  401.8 9.5 copy-start.29
  424.0 60.9 %copy-start.17 = (f32[512,1024]{1,0:T(8,128)}, f32[512,1024]{1,0:T(8,128)S(1)}, u32[]{:S(2)}) copy-start(f32[512,1024]{1,0:T(8,128)S(1)} %get-tuple-element.84) | copy-start | bytes 6291460
  424.0 60.9 %copy-start.52 = (f32[512]{0:T(512)}, f32[512]{0:T(512)S(1)}, u32[]{:S(2)}) copy-start(f32[512]{0:T(512)S(1)} %broadcast_multiply_fusion.9) | copy-start | bytes 6148
  424.4 60.6 %copy-start.75 = (f32[512]{0:T(512)}, f32[512]{0:T(512)S(1)}, u32[]{:S(2)}) copy-start(f32[512]{0:T(512)S(1)} %add_rsqrt_fusion.1) | copy-start | bytes 6148
  442.7 9.2 copy-start.22
  442.7 9.2 copy-start.46
  442.7 10.7 copy-start.66
  456.2 19.0 %copy-start.34 = (f32[512,1024]{1,0:T(8,128)}, f32[512,1024]{1,0:T(8,128)S(1)}, u32[]{:S(2)}) copy-start(f32[512,1024]{1,0:T(8,128)S(1)} %get-tuple-element.36) | copy-start | bytes 6291460
  475.2 9.7 copy-start.99
  502.8 12.6 %copy-start.6 = (bf16[512,1024]{0,1:T(8,128)(2,1)S(1)}, bf16[512,1024]{0,1:T(8,128)(2,1)}, u32[]{:S(2)}) copy-start(bf16[512,1024]{0,1:T(8,128)(2,1)} %copy-done.5) | copy-start | bytes 3145732
  516.9 11.1 copy-start.20
  537.4 18.8 %copy-start.38 = (f32[512,1024]{1,0:T(8,128)}, f32[512,1024]{1,0:T(8,128)S(1)}, u32[]{:S(2)}) copy-start(f32[512,1024]{1,0:T(8,128)S(1)} %get-tuple-element.32) | copy-start | bytes 6291460
  537.4 18.8 %copy-start.16 = (f32[512,1024]{1,0:T(8,128)S(1)}, f32[512,1024]{1,0:T(8,128)}, u32[]{:S(2)}) copy-start(f32[512,1024]{1,0:T(8,128)} %copy-done.15) | copy-start | bytes 6291460
  537.4 18.8 %copy-start.51 = (f32[512]{0:T(512)S(1)}, f32[512]{0:T(512)}, u32[]{:S(2)}) copy-start(f32[512]{0:T(512)} %copy-done.50) | copy-start | bytes 6148
  537.4 18.8 %copy-start.65 = (f32[1,1,1,1024]{3,1,2,0:T(1,128)S(1)}, f32[1,1,1,1024]{3,1,2,0:T(1,128)}, u32[]{:S(2)}) copy-start(f32[1,1,1,1024]{3,1,2,0:T(1,128)} %copy-done.64) | copy-start | bytes 12292
  537.4 18.8 %copy-start.74 = (f32[512]{0:T(512)S(1)}, f32[512]{0:T(512)}, u32[]{:S(2)}) copy-start(f32[512]{0:T(512)} %copy-done.73) | copy-start | bytes 6148
  556.2 9.2 copy-start.101
  572.8 12.4 copy-start.26
  585.1 12.6 %copy-start.4 = (bf16[512,1024]{0,1:T(8,128)(2,1)S(1)}, bf16[512,1024]{0,1:T(8,128)(2,1)}, u32[]{:S(2)}) copy-start(bf16[512,1024]{0,1:T(8,128)(2,1)} %copy-done.3) | copy-start | bytes 3145732
  601.9 25.2 %copy-start.23 = (bf16[16,64,512]{2,1,0:T(8,128)(2,1)}, bf16[16,64,512]{2,1,0:T(8,128)(2,1)S(1)}, u32[]{:S(2)}) copy-start(bf16[16,64,512]{2,1,0:T(8,128)(2,1)S(1)} %multiply_convert_fusion.6) | copy-start | bytes 3145732
  610.4 16.7 %copy-start.40 = (bf16[16,64,512]{2,1,0:T(8,128)(2,1)}, bf16[16,64,512]{2,1,0:T(8,128)(2,1)S(1)}, u32[]{:S(2)}) copy-start(bf16[16,64,512]{2,1,0:T(8,128)(2,1)S(1)} %convolution_convert_fusion.7) | copy-start | bytes 3145732
  664.9 498.0 %reduce-scatter.5.cloned.1.call-start = ((), (), s32[]{:S(2)}) async-start(), calls=%async_computation.7 | async-start | bytes 25952256 | tf_op jit(solution)/shard_map/reduce_scatter | solution.py:240
  673.5 9.1 copy-start.35
  716.4 516.9 %all-gather.10.cloned.1.call-start = ((), (), s32[]{:S(2)}) async-start(), calls=%async_computation.8 | async-start | bytes 3244032 | tf_op jit(solution)/shard_map/all_gather | solution.py:255
  1171.2 66.9 %all-to-all-start.1 = ((bf16[32,4,32,256]{3,2,1,0:T(8,128)(2,1)}), bf16[32,4,32,256]{3,2,1,0:T(8,128)(2,1)S(1)}, u32[]{:S(2)}, u32[]{:S(2)}) async-start(bf16[32,4,32,256]{3,2,1,0:T(8,128)(2,1)} %bitcast.168), calls=%async_computation.3 | async-start | bytes 4194304 | tf_op jit(solution)/shard_map/all_to_all | solution.py:269
  1175.7 60.7 %copy-start.44 = (f32[3,2,6,1024]{3,1,2,0:T(2,128)S(1)}, f32[3,2,6,1024]{3,1,2,0:T(2,128)}, u32[]{:S(2)}) copy-start(f32[3,2,6,1024]{3,1,2,0:T(2,128)} %param.16) | copy-start | bytes 442372
  1175.7 60.9 %copy-start.45 = (f32[3,2,6,256]{3,1,2,0:T(2,128)S(1)}, f32[3,2,6,256]{3,1,2,0:T(2,128)}, u32[]{:S(2)}) copy-start(f32[3,2,6,256]{3,1,2,0:T(2,128)} %param.15) | copy-start | bytes 110596
  (63 other events, 393.4 us)
Sparse Core Ops, SparseCore 0:
  74.9 154.1 all-gather.5
  232.6 152.7 all-gather.7
  664.9 245.4 reduce-scatter.2
  917.8 244.9 reduce-scatter.4
  1166.2 67.1 all-gather.9
